TPU v7x, 32 devices: a whole 2x2x4 slice. The times are simulated.
32 devices in a mesh: aux: 8 (over z, x), lmo: 4 (over y, core).
Axes of the slice: x: 2, y: 2, z: 4, core: 2. Of those that a mesh axis runs over, the one named last changes fastest.
Arguments:
- aux_ints: bfloat16 [256, 768, 768], P(('aux', 'lmo')), may hold values from -6 to 6
- lmo_coef: bfloat16 [128, 384], P(('aux', 'lmo')), may hold values from -0.3125 to 0.3125
- ao_domain: int32 [128, 3], replicated, may hold values from 0 to 5, as said below
- ao_count: int32 [128], replicated, may hold values from 1 to 3
- pao_domain: int32 [128, 3], replicated, may hold values from 0 to 5, as said below
- pao_count: int32 [128], replicated, may hold values from 1 to 3, as said below
- owner_order: int32 [128], replicated, may hold values from 0 to 127, as said below
- pao_coef: bfloat16 [128, 384, 256], P(('aux', 'lmo')), may hold values from -0.3125 to 0.3125
Outputs:
- pair_ints: bfloat16 [128, 256, 256], P(('aux', 'lmo'))
- pair_metric: float32 [128, 256, 256], P(('aux', 'lmo'))
Inputs may be any that keep to these rules, and one draw needn't show every extreme that they name: `ao_domain`: each row holds 3 different block numbers; slots from ao_count on are unused. `pao_domain`: each row holds 3 different block numbers; slots from pao_count on are unused. `pao_count`: the LMOs of the 4 owner slots of one device use together at most 8 PAO block slots, and those of some device use exactly 8. `owner_order`: every LMO stands in exactly one slot.
All inputs are finite; a program needn't handle non-finite values.
Results may differ from a plain program's by a relative error of at most 0.0049.
Values may be sent and summed in bfloat16 or wider, within the bound.
A program may use at most 128 MiB of HBM per device.

v0:
```python
import functools

import jax
import jax.numpy as jnp
from jax import lax
from jax.experimental import pallas as pl
from jax.experimental.pallas import tpu as pltpu
from jax.sharding import PartitionSpec as P

BLK = 128
DB = 3
PB = 3
PARTS = 1
USED = 8
MESH = pl.DeviceIdType.MESH


def exchange(
    n_aux, n_lmo,
    aux_hbm, lmo_ref, ao_dom, ao_cnt, pao_dom, pao_cnt, order, recv,
    aux, coef_all, coef32, dense, half, tab, send,
    aux_sem, coef_send, coef_recv, out_send, out_recv, own_sem,
):
    dev = n_aux * n_lmo
    rows, ao, _ = aux_hbm.shape
    blocks = ao // BLK
    per = lmo_ref.shape[0]
    lmos = per * dev
    me = lax.axis_index("aux") * n_lmo + lax.axis_index("lmo")

    def coords(d):
        return (d // n_lmo, lax.rem(d, n_lmo))

    def partner(t):
        return lax.rem(me + t, dev)

    def load(p):
        return pltpu.make_async_copy(aux_hbm.at[p], aux.at[p], aux_sem.at[p])

    for p in range(rows):
        load(p).start()

    barrier = pltpu.get_barrier_semaphore()

    @pl.loop(1, dev)
    def _(t):
        pl.semaphore_signal(barrier, inc=1, device_id=coords(partner(t)), device_id_type=MESH)

    pl.semaphore_wait(barrier, dev - 1)

    def coef_copy(slot, d):
        return pltpu.make_async_remote_copy(
            src_ref=lmo_ref, dst_ref=coef_all.at[slot],
            send_sem=coef_send.at[d], recv_sem=coef_recv.at[slot],
            device_id=coords(d), device_id_type=MESH,
        )

    @pl.loop(1, dev)
    def _(t):
        coef_copy(me, partner(t)).start()

    coef_all[me] = lmo_ref[...]

    @pl.loop(0, dev)
    def _(d):
        lmo = [order[d * per + j] for j in range(per)]
        cnt = [pao_cnt[i] for i in lmo]
        for s in range(USED):
            i, k = lmo[0], jnp.int32(s)
            start = jnp.int32(0)
            for j in range(1, per):
                start = start + cnt[j - 1]
                past = s >= start
                i = jnp.where(past, lmo[j], i)
                k = jnp.where(past, s - start, k)
            tab[d * USED + s] = i * blocks + pao_dom[jnp.minimum(k, PB - 1), i]

    @pl.loop(1, dev)
    def _(t):
        d = partner(t)
        coef_copy(d, d).wait_recv()

    for d in range(dev):
        coef32[d * per:(d + 1) * per, :] = coef_all[d].astype(jnp.float32)

    eye = lax.broadcasted_iota(jnp.int32, (lmos, lmos), 0) == lax.broadcasted_iota(
        jnp.int32, (lmos, lmos), 1
    )
    where_to = []
    for k in range(DB):
        block = jnp.where(ao_cnt[...] > k, ao_dom[k:k + 1, :], -1).astype(jnp.float32)
        column = jnp.sum(jnp.where(eye, block, 0.0), axis=1, keepdims=True)
        where_to.append(jnp.broadcast_to(column, (lmos, BLK)))
    for b in range(blocks):
        total = jnp.zeros((lmos, BLK), jnp.float32)
        for k in range(DB):
            total = jnp.where(where_to[k] == b, coef32[:, k * BLK:(k + 1) * BLK], total)
        dense[:, b * BLK:(b + 1) * BLK] = total.astype(jnp.bfloat16)

    flat = half.reshape(lmos * blocks * rows, BLK)
    chunk = rows // PARTS

    def transform(g):
        for p in range(g * chunk, (g + 1) * chunk):
            load(p).wait()
        out = lax.dot_general(
            dense[...], aux[g * chunk:(g + 1) * chunk].reshape(chunk * ao, ao),
            (((1,), (1,)), ((), ())), preferred_element_type=jnp.float32,
        )
        for q in range(chunk):
            for b in range(blocks):
                first = q * ao + b * BLK
                flat[pl.ds(b * rows + g * chunk + q, lmos, stride=blocks * rows), :] = (
                    out[:, first:first + BLK]
                )

    def pack(g, d):
        for s in range(USED):
            row = tab[d * USED + s]
            send[g, d, s] = half[row, g * chunk:(g + 1) * chunk, :].astype(jnp.bfloat16)

    def out_copy(g, slot, d):
        return pltpu.make_async_remote_copy(
            src_ref=send.at[g, d], dst_ref=recv.at[g, slot],
            send_sem=out_send.at[g, d], recv_sem=out_recv.at[g, slot],
            device_id=coords(d), device_id_type=MESH,
        )

    def own_copy(g):
        return pltpu.make_async_copy(send.at[g, me], recv.at[g, me], own_sem.at[g])

    for g in range(PARTS):
        transform(g)
        pack(g, partner(1))

        @pl.loop(1, dev)
        def _(t):
            pack(g, partner(t + 1))
            out_copy(g, me, partner(t)).start()

        own_copy(g).start()

    @pl.loop(1, dev)
    def _(t):
        d = partner(t)
        coef_copy(d, d).wait_send()
        for g in range(PARTS):
            out_copy(g, d, d).wait_send()
            out_copy(g, d, d).wait_recv()

    for g in range(PARTS):
        own_copy(g).wait()


def contract(n_lmo, per, recv, coef, pao_cnt, order, pair, metric, pair_out, metric_out, sem):
    me = lax.axis_index("aux") * n_lmo + lax.axis_index("lmo")
    _, dev, _, chunk, _ = recv.shape
    rows = PARTS * chunk
    start = jnp.int32(0)
    copies = []
    for g in range(per):
        count = pao_cnt[order[me * per + g]]
        tiles = []
        for k in range(PB):
            slot = jnp.minimum(start + k, USED - 1)
            tile = jnp.concatenate(
                [recv[h, :, slot].astype(jnp.float32) for h in range(PARTS)], axis=1
            ).reshape(dev * rows, BLK)
            tiles.append(jnp.where(k < count, tile, 0.0).astype(jnp.bfloat16))
        start = start + count
        row = jnp.dot(
            jnp.concatenate(tiles, axis=1), coef[g], preferred_element_type=jnp.float32
        ).astype(jnp.bfloat16)
        pair_out[g] = row
        metric_out[g] = lax.dot_general(
            row, row, (((0,), (0,)), ((), ())), preferred_element_type=jnp.float32
        ) / (dev * rows)
        for c, (src, dst) in enumerate(((pair_out, pair), (metric_out, metric))):
            copies.append(pltpu.make_async_copy(src.at[g], dst.at[g], sem.at[g, c]))
            copies[-1].start()
    for copy in copies:
        copy.wait()


def shards(mesh, aux_ints, lmo_coef, ao_domain, ao_count, pao_domain, pao_count, owner_order, pao_coef):
    n_aux, n_lmo = mesh.shape["aux"], mesh.shape["lmo"]
    dev = n_aux * n_lmo
    rows, ao, _ = aux_ints.shape
    blocks = ao // BLK
    per = lmo_coef.shape[0]
    lmos = per * dev
    npao = pao_coef.shape[2]
    vmem = pl.BlockSpec(memory_space=pltpu.VMEM)
    smem = pl.BlockSpec(memory_space=pltpu.SMEM)
    anywhere = pl.BlockSpec(memory_space=pl.ANY)
    recv = pl.pallas_call(
        functools.partial(exchange, n_aux, n_lmo),
        out_shape=jax.ShapeDtypeStruct((PARTS, dev, USED, rows // PARTS, BLK), jnp.bfloat16),
        in_specs=[anywhere, vmem, vmem, vmem, smem, smem, smem],
        out_specs=anywhere,
        scratch_shapes=[
            pltpu.VMEM((rows, ao, ao), jnp.bfloat16),
            pltpu.VMEM((dev, per, DB * BLK), jnp.bfloat16),
            pltpu.VMEM((lmos, DB * BLK), jnp.float32),
            pltpu.VMEM((lmos, ao), jnp.bfloat16),
            pltpu.VMEM((lmos * blocks, rows, BLK), jnp.float32),
            pltpu.SMEM((dev * USED,), jnp.int32),
            pltpu.VMEM((PARTS, dev, USED, rows // PARTS, BLK), jnp.bfloat16),
            pltpu.SemaphoreType.DMA((rows,)),
            pltpu.SemaphoreType.DMA((dev,)),
            pltpu.SemaphoreType.DMA((dev,)),
            pltpu.SemaphoreType.DMA((PARTS, dev)),
            pltpu.SemaphoreType.DMA((PARTS, dev)),
            pltpu.SemaphoreType.DMA((PARTS,)),
        ],
        compiler_params=pltpu.CompilerParams(
            collective_id=0, has_side_effects=True, vmem_limit_bytes=60 * 2**20
        ),
        name="exchange",
    )(aux_ints, lmo_coef, ao_domain.T, ao_count.reshape(1, lmos), pao_domain.T, pao_count, owner_order)
    pair, metric = pl.pallas_call(
        functools.partial(contract, n_lmo, per),
        out_shape=(
            jax.ShapeDtypeStruct((per, dev * rows, npao), jnp.bfloat16),
            jax.ShapeDtypeStruct((per, npao, npao), jnp.float32),
        ),
        in_specs=[
            vmem,
            vmem,
            smem,
            smem,
        ],
        out_specs=(anywhere, anywhere),
        scratch_shapes=[
            pltpu.VMEM((per, dev * rows, npao), jnp.bfloat16),
            pltpu.VMEM((per, npao, npao), jnp.float32),
            pltpu.SemaphoreType.DMA((per, 2)),
        ],
        name="contract",
    )(recv, pao_coef, pao_count, owner_order)
    return pair, metric


def solution(mesh):
    split = ("aux", "lmo")
    placed = (P(split, None, None), P(split, None), P(), P(), P(), P(), P(), P(split, None, None))
    return jax.shard_map(
        functools.partial(shards, mesh),
        mesh=mesh,
        in_specs=placed,
        out_specs=(P(split, None, None), P(split, None, None)),
        check_vma=False,
    )
```

profile of v0, /device:TPU:11, one launch (start us, length us, event | category | flops | bytes accessed | tf_op | source)
XLA Modules:
  0.0 33.8 jit_solution(6275170331936301732)
XLA Ops:
  0.6 29.5 %exchange.1.recv = bf16[1,32,8,8,128]{4,3,2,1,0:T(8,128)(2,1)} custom-call(bf16[8,768,768]{2,1,0:T(8,128)(2,1)} %aux_hbm.1, bf16[4,384]{1,0:T(4,128)(2,1)} %lmo_ref.1, s32[3,128]{1,0:T(4,128)} %bitcast.3, s32[1,128]{1,0:T(1,128)} %bitcast.5, s32[3,128]{1,0:T(4,128)} %bitcast.4, s32[128]{0:T(128)} %pao_cnt.3, s32[128]{0:T(128)} %order.3), custom_call_target="tpu_custom_call" | custom-call | tf_op jit(solution)/shard_map/exchange/pallas_call | solution.py:196
  30.2 3.7 %contract.1 = (bf16[4,256,256]{2,1,0:T(8,128)(2,1)}, f32[4,256,256]{2,1,0:T(8,128)}) custom-call(bf16[1,32,8,8,128]{4,3,2,1,0:T(8,128)(2,1)} %exchange.1.recv, bf16[4,384,256]{2,1,0:T(8,128)(2,1)} %coef.1, s32[128]{0:T(128)} %pao_cnt.3, s32[128]{0:T(128)} %order.3), custom_call_target="tpu_custom_call" | custom-call | tf_op jit(solution)/shard_map/contract/pallas_call | solution.py:221
where the time goes:
time: 34 us; the launch traced here: 33.8 us
  Pallas kernels  33.2 us (98%)
  between operations  0.64 us (2%)
    pallas_call x1, Pallas kernels, shards(): pl.pallas_call(functools.partial(exchange, n_aux, n_lmo), out_shape=jax.S...  29.5 us
    pallas_call x1, Pallas kernels, shards(): pl.pallas_call(functools.partial(contract, n_lmo, per), out_shape=(jax.Sh...  3.66 us

commit v1 on v0

v1 whole, which is shorter than its diff:
```python
import functools

import jax
import jax.numpy as jnp
from jax import lax
from jax.experimental import pallas as pl
from jax.experimental.pallas import tpu as pltpu
from jax.sharding import PartitionSpec as P

BLK = 128
DB = 3
PB = 3
USED = 8
MESH = pl.DeviceIdType.MESH


def exchange(
    n_aux, n_lmo, plane,
    aux_hbm, lmo_hbm, ao_dom_hbm, ao_cnt_hbm, pao_dom_hbm, pao_cnt_hbm, order_hbm, recv,
    aux, aux_t, lmo_ref, ao_dom, ao_cnt, pao_dom, pao_cnt, order,
    coef_all, coef32, dense, half, tab, send,
    aux_sem, in_sem, entered, coef_send, coef_recv, out_send, out_recv,
):
    dev = n_aux * n_lmo
    rows, ao, _ = aux_hbm.shape
    blocks = ao // BLK
    per = lmo_hbm.shape[0]
    lmos = per * dev
    planes = dev // plane
    me = lax.axis_index("aux") * n_lmo + lax.axis_index("lmo")
    my_plane, seat = me // plane, lax.rem(me, plane)

    def coords(d):
        return (d // n_lmo, lax.rem(d, n_lmo))

    barrier = pltpu.get_barrier_semaphore()

    @pl.loop(me + 1, dev)
    def _(d):
        pl.semaphore_signal(barrier, inc=1, device_id=coords(d), device_id_type=MESH)

    small = [
        pltpu.make_async_copy(src, dst, in_sem.at[n])
        for n, (src, dst) in enumerate((
            (lmo_hbm, lmo_ref), (ao_dom_hbm, ao_dom), (ao_cnt_hbm, ao_cnt),
            (pao_dom_hbm, pao_dom), (pao_cnt_hbm, pao_cnt), (order_hbm, order),
        ))
    ]
    for copy in small:
        copy.start()

    def load(p):
        return pltpu.make_async_copy(aux_hbm.at[p], aux.at[p], aux_sem.at[p])

    for p in range(rows):
        load(p).start()

    def coef_copy(slot, d):
        return pltpu.make_async_remote_copy(
            src_ref=lmo_ref, dst_ref=coef_all.at[slot],
            send_sem=coef_send.at[d], recv_sem=coef_recv.at[slot],
            device_id=coords(d), device_id_type=MESH,
        )

    @pl.when(me > 0)
    def _():
        pl.semaphore_wait(barrier, me)

    @pl.loop(0, me)
    def _(d):
        pl.semaphore_signal(entered.at[me], inc=1, device_id=coords(d), device_id_type=MESH)

    small[0].wait()

    @pl.loop(0, me)
    def _(d):
        coef_copy(me, d).start()

    coef_all[me] = lmo_ref[...]
    for copy in small[1:]:
        copy.wait()

    def greet(first, last):
        @pl.loop(first, last)
        def _(d):
            pl.semaphore_wait(entered.at[d], 1)
            coef_copy(me, d).start()

    @pl.loop(0, dev)
    def _(d):
        lmo = [order[d * per + j] for j in range(per)]
        cnt = [pao_cnt[i] for i in lmo]
        for s in range(USED):
            i, k = lmo[0], jnp.int32(s)
            start = jnp.int32(0)
            for j in range(1, per):
                start = start + cnt[j - 1]
                past = s >= start
                i = jnp.where(past, lmo[j], i)
                k = jnp.where(past, s - start, k)
            tab[d * USED + s] = i * blocks + pao_dom[jnp.minimum(k, PB - 1), i]

    eye = lax.broadcasted_iota(jnp.int32, (lmos, lmos), 0) == lax.broadcasted_iota(
        jnp.int32, (lmos, lmos), 1
    )
    where_to = []
    for k in range(DB):
        block = jnp.where(ao_cnt[...] > k, ao_dom[k:k + 1, :], -1).astype(jnp.float32)
        column = jnp.sum(jnp.where(eye, block, 0.0), axis=1, keepdims=True)
        where_to.append(jnp.broadcast_to(column, (lmos, BLK)))

    later = dev - 1 - me
    for p in range(rows):
        load(p).wait()
        aux_t[p] = aux[p].T
        greet(me + 1 + later * p // rows, me + 1 + later * (p + 1) // rows)

    @pl.loop(0, me)
    def _(d):
        coef_copy(d, d).wait_recv()

    @pl.loop(me + 1, dev)
    def _(d):
        coef_copy(d, d).wait_recv()

    for d in range(dev):
        coef32[d * per:(d + 1) * per, :] = coef_all[d].astype(jnp.float32)
    for b in range(blocks):
        total = jnp.zeros((lmos, BLK), jnp.float32)
        for k in range(DB):
            total = jnp.where(where_to[k] == b, coef32[:, k * BLK:(k + 1) * BLK], total)
        dense[:, b * BLK:(b + 1) * BLK] = total.astype(jnp.bfloat16)

    flat = half.reshape(lmos * blocks * rows, BLK)
    wide = 2
    for p in range(rows):
        for b in range(0, blocks, wide):
            out = jnp.dot(
                dense[...], aux_t[p, :, b * BLK:(b + wide) * BLK],
                preferred_element_type=jnp.float32,
            )
            for c in range(wide):
                flat[pl.ds((b + c) * rows + p, lmos, stride=blocks * rows), :] = (
                    out[:, c * BLK:(c + 1) * BLK]
                )

    def packed(d, s):
        return half[tab[d * USED + s]].astype(jnp.bfloat16)

    def pack(d):
        for s in range(USED):
            send[d, s] = packed(d, s)

    def out_copy(slot, d):
        return pltpu.make_async_remote_copy(
            src_ref=send.at[d], dst_ref=recv.at[slot],
            send_sem=out_send.at[d], recv_sem=out_recv.at[slot],
            device_id=coords(d), device_id_type=MESH,
        )

    def target(t):
        i, j = t // plane, lax.rem(t, plane)
        own = i == planes - 1
        other = jnp.where(i >= my_plane, i + 1, i)
        return jnp.where(
            own,
            my_plane * plane + lax.rem(seat + 1 + j, plane),
            other * plane + lax.rem(seat + j, plane),
        )

    pack(target(0))

    @pl.loop(0, dev - 2)
    def _(t):
        pack(target(t + 1))
        out_copy(me, target(t)).start()

    for s in range(USED):
        recv[me, s] = packed(me, s)
    out_copy(me, target(dev - 2)).start()

    @pl.loop(0, dev - 1)
    def _(t):
        d = target(t)
        coef_copy(d, d).wait_send()
        out_copy(d, d).wait_send()

    @pl.loop(0, dev - 1)
    def _(t):
        d = target(t)
        out_copy(d, d).wait_recv()


def contract(n_lmo, per, recv, coef, pao_cnt, order, pair, metric, pair_out, metric_out, sem):
    me = lax.axis_index("aux") * n_lmo + lax.axis_index("lmo")
    dev, _, rows, _ = recv.shape
    start = jnp.int32(0)
    copies = []
    for g in range(per):
        count = pao_cnt[order[me * per + g]]
        tiles = []
        for k in range(PB):
            slot = jnp.minimum(start + k, USED - 1)
            tile = recv[:, slot].astype(jnp.float32).reshape(dev * rows, BLK)
            tiles.append(jnp.where(k < count, tile, 0.0).astype(jnp.bfloat16))
        start = start + count
        row = jnp.dot(
            jnp.concatenate(tiles, axis=1), coef[g], preferred_element_type=jnp.float32
        ).astype(jnp.bfloat16)
        pair_out[g] = row
        metric_out[g] = lax.dot_general(
            row, row, (((0,), (0,)), ((), ())), preferred_element_type=jnp.float32
        ) / (dev * rows)
        for c, (src, dst) in enumerate(((pair_out, pair), (metric_out, metric))):
            copies.append(pltpu.make_async_copy(src.at[g], dst.at[g], sem.at[g, c]))
            copies[-1].start()
    for copy in copies:
        copy.wait()


def shards(mesh, aux_ints, lmo_coef, ao_domain, ao_count, pao_domain, pao_count, owner_order, pao_coef):
    n_aux, n_lmo = mesh.shape["aux"], mesh.shape["lmo"]
    dev = n_aux * n_lmo
    rows, ao, _ = aux_ints.shape
    blocks = ao // BLK
    per = lmo_coef.shape[0]
    lmos = per * dev
    npao = pao_coef.shape[2]
    across = n_lmo // 2 if n_lmo % 2 == 0 and n_aux % (n_lmo // 2) == 0 else 1
    plane = across * n_lmo
    vmem = pl.BlockSpec(memory_space=pltpu.VMEM)
    smem = pl.BlockSpec(memory_space=pltpu.SMEM)
    anywhere = pl.BlockSpec(memory_space=pl.ANY)
    recv = pl.pallas_call(
        functools.partial(exchange, n_aux, n_lmo, plane),
        out_shape=pltpu.VMEM((dev, USED, rows, BLK), jnp.bfloat16),
        in_specs=[anywhere] * 7,
        out_specs=vmem,
        scratch_shapes=[
            pltpu.VMEM((rows, ao, ao), jnp.bfloat16),
            pltpu.VMEM((rows, ao, ao), jnp.bfloat16),
            pltpu.VMEM((per, DB * BLK), jnp.bfloat16),
            pltpu.VMEM((DB, lmos), jnp.int32),
            pltpu.VMEM((1, lmos), jnp.int32),
            pltpu.SMEM((PB, lmos), jnp.int32),
            pltpu.SMEM((lmos,), jnp.int32),
            pltpu.SMEM((lmos,), jnp.int32),
            pltpu.VMEM((dev, per, DB * BLK), jnp.bfloat16),
            pltpu.VMEM((lmos, DB * BLK), jnp.float32),
            pltpu.VMEM((lmos, ao), jnp.bfloat16),
            pltpu.VMEM((lmos * blocks, rows, BLK), jnp.float32),
            pltpu.SMEM((dev * USED,), jnp.int32),
            pltpu.VMEM((dev, USED, rows, BLK), jnp.bfloat16),
            pltpu.SemaphoreType.DMA((rows,)),
            pltpu.SemaphoreType.DMA((6,)),
            pltpu.SemaphoreType.REGULAR((dev,)),
            pltpu.SemaphoreType.DMA((dev,)),
            pltpu.SemaphoreType.DMA((dev,)),
            pltpu.SemaphoreType.DMA((dev,)),
            pltpu.SemaphoreType.DMA((dev,)),
        ],
        compiler_params=pltpu.CompilerParams(
            collective_id=0, has_side_effects=True, vmem_limit_bytes=48 * 2**20
        ),
        name="exchange",
    )(*(
        pltpu.with_memory_space_constraint(x, pltpu.HBM)
        for x in (aux_ints, lmo_coef, ao_domain.T, ao_count.reshape(1, lmos), pao_domain.T, pao_count, owner_order)
    ))
    pair, metric = pl.pallas_call(
        functools.partial(contract, n_lmo, per),
        out_shape=(
            jax.ShapeDtypeStruct((per, dev * rows, npao), jnp.bfloat16),
            jax.ShapeDtypeStruct((per, npao, npao), jnp.float32),
        ),
        in_specs=[vmem, vmem, smem, smem],
        out_specs=(anywhere, anywhere),
        scratch_shapes=[
            pltpu.VMEM((per, dev * rows, npao), jnp.bfloat16),
            pltpu.VMEM((per, npao, npao), jnp.float32),
            pltpu.SemaphoreType.DMA((per, 2)),
        ],
        compiler_params=pltpu.CompilerParams(vmem_limit_bytes=24 * 2**20),
        name="contract",
    )(recv, pao_coef, pao_count, owner_order)
    return pair, metric


def solution(mesh):
    split = ("aux", "lmo")
    placed = (P(split, None, None), P(split, None), P(), P(), P(), P(), P(), P(split, None, None))
    return jax.shard_map(
        functools.partial(shards, mesh),
        mesh=mesh,
        in_specs=placed,
        out_specs=(P(split, None, None), P(split, None, None)),
        check_vma=False,
    )
```

time: 34 us -> 32.6 us (0.959)
  the two profiles are of different devices: /device:TPU:11 before, /device:TPU:13 now
where the time goes in v1:
time: 32.6 us; the launch traced here: 32.4 us
  Pallas kernels  31.7 us (97%)
  between operations  0.69 us (2%)
    pallas_call x1, Pallas kernels, shards(): pl.pallas_call(functools.partial(exchange, n_aux, n_lmo, plane), out_shap...  28.9 us
    pallas_call x1, Pallas kernels, shards(): pl.pallas_call(functools.partial(contract, n_lmo, per), out_shape=(jax.Sh...  2.89 us

profile of v1, /device:TPU:13, one launch (start us, length us, event | category | flops | bytes accessed | tf_op | source)
XLA Modules:
  0.0 32.4 jit_solution(2379064701083509244)
XLA Ops:
  0.6 0.0 copy-start.2
  0.6 0.0 copy-start.1
  0.7 0.0 copy-start
  0.7 28.9 %exchange.1.recv = bf16[32,8,8,128]{3,2,1,0:T(8,128)(2,1)S(1)} custom-call(bf16[8,768,768]{2,1,0:T(8,128)(2,1)} %aux_hbm.1, bf16[4,384]{1,0:T(4,128)(2,1)} %lmo_hbm.1, s32[3,128]{1,0:T(4,128)} %bitcast.3, s32[1,128]{1,0:T(1,128)} %bitcast.5, s32[3,128]{1,0:T(4,128)} %bitcast.4, s32[128]{0:T(128)} %pao_cnt.1, s32[128]{0:T(128)} %order.1), custom_call_target="tpu_custom_call" | custom-call | tf_op jit(solution)/shard_map/exchange/pallas_call | solution.py:234
  29.5 0.0 copy-done.2
  29.5 0.0 copy-done.1
  29.5 0.0 copy-done
  29.6 2.9 %contract.1 = (bf16[4,256,256]{2,1,0:T(8,128)(2,1)}, f32[4,256,256]{2,1,0:T(8,128)}) custom-call(bf16[32,8,8,128]{3,2,1,0:T(8,128)(2,1)S(1)} %exchange.1.recv, bf16[4,384,256]{2,1,0:T(8,128)(2,1)S(1)} %copy-done, s32[128]{0:T(128)S(1)} %copy-done.1, s32[128]{0:T(128)S(1)} %copy-done.2), custom_call_target="tpu_custom_call" | custom-call | tf_op jit(solution)/shard_map/contract/pallas_call | solution.py:270
Async XLA Ops:
  0.6 28.9 %copy-start.2 = (s32[128]{0:T(128)S(1)}, s32[128]{0:T(128)}, u32[]{:S(2)}) copy-start(s32[128]{0:T(128)} %order.1) | copy-start | bytes 1540
  0.6 28.9 %copy-start.1 = (s32[128]{0:T(128)S(1)}, s32[128]{0:T(128)}, u32[]{:S(2)}) copy-start(s32[128]{0:T(128)} %pao_cnt.1) | copy-start | bytes 1540
  0.7 28.9 %copy-start = (bf16[4,384,256]{2,1,0:T(8,128)(2,1)S(1)}, bf16[4,384,256]{2,1,0:T(8,128)(2,1)}, u32[]{:S(2)}) copy-start(bf16[4,384,256]{2,1,0:T(8,128)(2,1)} %coef.1) | copy-start | bytes 2359300

commit v2 on v1

--- a/solution.py
+++ b/solution.py
@@ -18,7 +18,7 @@
     n_aux, n_lmo, plane,
     aux_hbm, lmo_hbm, ao_dom_hbm, ao_cnt_hbm, pao_dom_hbm, pao_cnt_hbm, order_hbm, recv,
     aux, aux_t, lmo_ref, ao_dom, ao_cnt, pao_dom, pao_cnt, order,
-    coef_all, coef32, dense, half, tab, send,
+    coef_all, coef32, dense, half, send,
     aux_sem, in_sem, entered, coef_send, coef_recv, out_send, out_recv,
 ):
     dev = n_aux * n_lmo
@@ -86,20 +86,6 @@
             pl.semaphore_wait(entered.at[d], 1)
             coef_copy(me, d).start()
 
-    @pl.loop(0, dev)
-    def _(d):
-        lmo = [order[d * per + j] for j in range(per)]
-        cnt = [pao_cnt[i] for i in lmo]
-        for s in range(USED):
-            i, k = lmo[0], jnp.int32(s)
-            start = jnp.int32(0)
-            for j in range(1, per):
-                start = start + cnt[j - 1]
-                past = s >= start
-                i = jnp.where(past, lmo[j], i)
-                k = jnp.where(past, s - start, k)
-            tab[d * USED + s] = i * blocks + pao_dom[jnp.minimum(k, PB - 1), i]
-
     eye = lax.broadcasted_iota(jnp.int32, (lmos, lmos), 0) == lax.broadcasted_iota(
         jnp.int32, (lmos, lmos), 1
     )
@@ -109,11 +95,15 @@
         column = jnp.sum(jnp.where(eye, block, 0.0), axis=1, keepdims=True)
         where_to.append(jnp.broadcast_to(column, (lmos, BLK)))
 
-    later = dev - 1 - me
-    for p in range(rows):
-        load(p).wait()
-        aux_t[p] = aux[p].T
-        greet(me + 1 + later * p // rows, me + 1 + later * (p + 1) // rows)
+    first = me + 1
+    for p in range(max(rows, planes)):
+        if p < planes:
+            last = jnp.minimum(first + plane, dev)
+            greet(first, last)
+            first = last
+        if p < rows:
+            load(p).wait()
+            aux_t[p] = aux[p].T
 
     @pl.loop(0, me)
     def _(d):
@@ -144,12 +134,19 @@
                     out[:, c * BLK:(c + 1) * BLK]
                 )
 
-    def packed(d, s):
-        return half[tab[d * USED + s]].astype(jnp.bfloat16)
-
-    def pack(d):
+    def pack(d, dst):
+        lmo = [order[d * per + j] for j in range(per)]
+        cnt = [pao_cnt[i] for i in lmo]
         for s in range(USED):
-            send[d, s] = packed(d, s)
+            i, k = lmo[0], jnp.int32(s)
+            start = jnp.int32(0)
+            for j in range(1, per):
+                start = start + cnt[j - 1]
+                past = s >= start
+                i = jnp.where(past, lmo[j], i)
+                k = jnp.where(past, s - start, k)
+            row = i * blocks + pao_dom[jnp.minimum(k, PB - 1), i]
+            dst[s] = half[row].astype(jnp.bfloat16)
 
     def out_copy(slot, d):
         return pltpu.make_async_remote_copy(
@@ -168,15 +165,14 @@
             other * plane + lax.rem(seat + j, plane),
         )
 
-    pack(target(0))
+    pack(target(0), send.at[target(0)])
 
     @pl.loop(0, dev - 2)
     def _(t):
-        pack(target(t + 1))
+        pack(target(t + 1), send.at[target(t + 1)])
         out_copy(me, target(t)).start()
 
-    for s in range(USED):
-        recv[me, s] = packed(me, s)
+    pack(me, recv.at[me])
     out_copy(me, target(dev - 2)).start()
 
     @pl.loop(0, dev - 1)
@@ -249,7 +245,6 @@
             pltpu.VMEM((lmos, DB * BLK), jnp.float32),
             pltpu.VMEM((lmos, ao), jnp.bfloat16),
             pltpu.VMEM((lmos * blocks, rows, BLK), jnp.float32),
-            pltpu.SMEM((dev * USED,), jnp.int32),
             pltpu.VMEM((dev, USED, rows, BLK), jnp.bfloat16),
             pltpu.SemaphoreType.DMA((rows,)),
             pltpu.SemaphoreType.DMA((6,)),

time: 32.6 us -> 30.8 us (0.945)
  Pallas kernels: 31.7 us -> 29.9 us
    pallas_call x1, Pallas kernels: 28.9 us -> 27.1 us  [shards(): pl.pallas_call(functools.partial(exchange, n_aux, n_lmo, plane), out_shap...]
where the time goes in v2:
time: 30.8 us; the launch traced here: 30.6 us
  Pallas kernels  29.9 us (97%)
  between operations  0.69 us (2%)
    pallas_call x1, Pallas kernels, shards(): pl.pallas_call(functools.partial(exchange, n_aux, n_lmo, plane), out_shap...  27.1 us
    pallas_call x1, Pallas kernels, shards(): pl.pallas_call(functools.partial(contract, n_lmo, per), out_shape=(jax.Sh...  2.89 us

profile of v2, /device:TPU:13, one launch (start us, length us, event | category | flops | bytes accessed | tf_op | source)
XLA Modules:
  0.0 30.6 jit_solution(10142671283543453153)
XLA Ops:
  0.6 0.0 copy-start.2
  0.6 0.0 copy-start.1
  0.7 0.0 copy-start
  0.7 27.1 %exchange.1.recv = bf16[32,8,8,128]{3,2,1,0:T(8,128)(2,1)S(1)} custom-call(bf16[8,768,768]{2,1,0:T(8,128)(2,1)} %aux_hbm.1, bf16[4,384]{1,0:T(4,128)(2,1)} %lmo_hbm.1, s32[3,128]{1,0:T(4,128)} %bitcast.3, s32[1,128]{1,0:T(1,128)} %bitcast.5, s32[3,128]{1,0:T(4,128)} %bitcast.4, s32[128]{0:T(128)} %pao_cnt.1, s32[128]{0:T(128)} %order.1), custom_call_target="tpu_custom_call" | custom-call | tf_op jit(solution)/shard_map/exchange/pallas_call | solution.py:230
  27.7 0.0 copy-done.2
  27.7 0.0 copy-done.1
  27.7 0.0 copy-done
  27.8 2.9 %contract.1 = (bf16[4,256,256]{2,1,0:T(8,128)(2,1)}, f32[4,256,256]{2,1,0:T(8,128)}) custom-call(bf16[32,8,8,128]{3,2,1,0:T(8,128)(2,1)S(1)} %exchange.1.recv, bf16[4,384,256]{2,1,0:T(8,128)(2,1)S(1)} %copy-done, s32[128]{0:T(128)S(1)} %copy-done.1, s32[128]{0:T(128)S(1)} %copy-done.2), custom_call_target="tpu_custom_call" | custom-call | tf_op jit(solution)/shard_map/contract/pallas_call | solution.py:265
Async XLA Ops:
  0.6 27.1 %copy-start.2 = (s32[128]{0:T(128)S(1)}, s32[128]{0:T(128)}, u32[]{:S(2)}) copy-start(s32[128]{0:T(128)} %order.1) | copy-start | bytes 1540
  0.6 27.1 %copy-start.1 = (s32[128]{0:T(128)S(1)}, s32[128]{0:T(128)}, u32[]{:S(2)}) copy-start(s32[128]{0:T(128)} %pao_cnt.1) | copy-start | bytes 1540
  0.7 27.1 %copy-start = (bf16[4,384,256]{2,1,0:T(8,128)(2,1)S(1)}, bf16[4,384,256]{2,1,0:T(8,128)(2,1)}, u32[]{:S(2)}) copy-start(bf16[4,384,256]{2,1,0:T(8,128)(2,1)} %coef.1) | copy-start | bytes 2359300

commit v3 on v2

--- a/solution.py
+++ b/solution.py
@@ -16,10 +16,10 @@
 
 def exchange(
     n_aux, n_lmo, plane,
-    aux_hbm, lmo_hbm, ao_dom_hbm, ao_cnt_hbm, pao_dom_hbm, pao_cnt_hbm, order_hbm, recv,
+    aux_hbm, lmo_hbm, ao_dom_hbm, ao_cnt_hbm, pao_dom_hbm, pao_cnt_hbm, order_hbm, pao_hbm, pair,
     aux, aux_t, lmo_ref, ao_dom, ao_cnt, pao_dom, pao_cnt, order,
-    coef_all, coef32, dense, half, send,
-    aux_sem, in_sem, entered, coef_send, coef_recv, out_send, out_recv,
+    coef_all, coef32, dense, half, send, recv, pao, pao_slots,
+    aux_sem, in_sem, pao_sem, entered, coef_send, coef_recv, out_send, out_recv,
 ):
     dev = n_aux * n_lmo
     rows, ao, _ = aux_hbm.shape
@@ -27,6 +27,7 @@
     per = lmo_hbm.shape[0]
     lmos = per * dev
     planes = dev // plane
+    pitch = half.shape[0] // lmos
     me = lax.axis_index("aux") * n_lmo + lax.axis_index("lmo")
     my_plane, seat = me // plane, lax.rem(me, plane)
 
@@ -54,6 +55,8 @@
 
     for p in range(rows):
         load(p).start()
+    pao_load = pltpu.make_async_copy(pao_hbm, pao, pao_sem)
+    pao_load.start()
 
     def coef_copy(slot, d):
         return pltpu.make_async_remote_copy(
@@ -121,7 +124,6 @@
             total = jnp.where(where_to[k] == b, coef32[:, k * BLK:(k + 1) * BLK], total)
         dense[:, b * BLK:(b + 1) * BLK] = total.astype(jnp.bfloat16)
 
-    flat = half.reshape(lmos * blocks * rows, BLK)
     wide = 2
     for p in range(rows):
         for b in range(0, blocks, wide):
@@ -130,7 +132,7 @@
                 preferred_element_type=jnp.float32,
             )
             for c in range(wide):
-                flat[pl.ds((b + c) * rows + p, lmos, stride=blocks * rows), :] = (
+                half[pl.ds((b + c) * rows + p, lmos, stride=pitch), :] = (
                     out[:, c * BLK:(c + 1) * BLK]
                 )
 
@@ -145,8 +147,8 @@
                 past = s >= start
                 i = jnp.where(past, lmo[j], i)
                 k = jnp.where(past, s - start, k)
-            row = i * blocks + pao_dom[jnp.minimum(k, PB - 1), i]
-            dst[s] = half[row].astype(jnp.bfloat16)
+            row = i * pitch + pao_dom[jnp.minimum(k, PB - 1), i] * rows
+            dst[s] = half[pl.ds(row, rows), :].astype(jnp.bfloat16)
 
     def out_copy(slot, d):
         return pltpu.make_async_remote_copy(
@@ -181,35 +183,57 @@
         coef_copy(d, d).wait_send()
         out_copy(d, d).wait_send()
 
-    @pl.loop(0, dev - 1)
-    def _(t):
-        d = target(t)
-        out_copy(d, d).wait_recv()
-
-
-def contract(n_lmo, per, recv, coef, pao_cnt, order, pair, metric, pair_out, metric_out, sem):
-    me = lax.axis_index("aux") * n_lmo + lax.axis_index("lmo")
-    dev, _, rows, _ = recv.shape
+    npao = pao.shape[3]
+    pao_load.wait()
     start = jnp.int32(0)
-    copies = []
     for g in range(per):
         count = pao_cnt[order[me * per + g]]
-        tiles = []
-        for k in range(PB):
-            slot = jnp.minimum(start + k, USED - 1)
-            tile = recv[:, slot].astype(jnp.float32).reshape(dev * rows, BLK)
-            tiles.append(jnp.where(k < count, tile, 0.0).astype(jnp.bfloat16))
+        for s in range(USED):
+            k = s - start
+            tile = pao[g, jnp.clip(k, 0, PB - 1)]
+            pao_slots[s * BLK:(s + 1) * BLK, g * npao:(g + 1) * npao] = jnp.where(
+                (k >= 0) & (k < count), tile, jnp.zeros_like(tile)
+            )
         start = start + count
-        row = jnp.dot(
-            jnp.concatenate(tiles, axis=1), coef[g], preferred_element_type=jnp.float32
-        ).astype(jnp.bfloat16)
-        pair_out[g] = row
-        metric_out[g] = lax.dot_general(
+
+    def project(i):
+        @pl.loop(0, plane)
+        def _(j):
+            d = i * plane + j
+
+            @pl.when(d != me)
+            def _():
+                out_copy(d, d).wait_recv()
+
+        first = pl.multiple_of(i * plane, plane)
+        here = jnp.concatenate([
+            recv[pl.ds(first, plane), s].astype(jnp.float32).reshape(plane * rows, BLK).astype(jnp.bfloat16)
+            for s in range(USED)
+        ], axis=1)
+        to = pl.multiple_of(i * (plane * rows), plane * rows)
+        for g in range(per):
+            pair[g, pl.ds(to, plane * rows), :] = jnp.dot(
+                here, pao_slots[:, g * npao:(g + 1) * npao], preferred_element_type=jnp.float32
+            ).astype(jnp.bfloat16)
+
+    project(jnp.where(my_plane == 0, 1, 0) if planes > 1 else my_plane)
+    if planes > 1:
+        project(my_plane)
+    for i in range(1, planes - 1):
+        project(jnp.where(i >= my_plane, i + 1, i))
+
+
+def contract(pair, pair_out, metric_out, metric, pair_sem, metric_sem):
+    per, total, _ = pair.shape
+    copies = [pltpu.make_async_copy(pair, pair_out, pair_sem)]
+    copies[0].start()
+    for g in range(per):
+        row = pair[g]
+        metric[g] = lax.dot_general(
             row, row, (((0,), (0,)), ((), ())), preferred_element_type=jnp.float32
-        ) / (dev * rows)
-        for c, (src, dst) in enumerate(((pair_out, pair), (metric_out, metric))):
-            copies.append(pltpu.make_async_copy(src.at[g], dst.at[g], sem.at[g, c]))
-            copies[-1].start()
+        ) / total
+        copies.append(pltpu.make_async_copy(metric.at[g], metric_out.at[g], metric_sem.at[g]))
+        copies[-1].start()
     for copy in copies:
         copy.wait()
 
@@ -225,12 +249,11 @@
     across = n_lmo // 2 if n_lmo % 2 == 0 and n_aux % (n_lmo // 2) == 0 else 1
     plane = across * n_lmo
     vmem = pl.BlockSpec(memory_space=pltpu.VMEM)
-    smem = pl.BlockSpec(memory_space=pltpu.SMEM)
     anywhere = pl.BlockSpec(memory_space=pl.ANY)
-    recv = pl.pallas_call(
+    pair = pl.pallas_call(
         functools.partial(exchange, n_aux, n_lmo, plane),
-        out_shape=pltpu.VMEM((dev, USED, rows, BLK), jnp.bfloat16),
-        in_specs=[anywhere] * 7,
+        out_shape=pltpu.VMEM((per, dev * rows, npao), jnp.bfloat16),
+        in_specs=[anywhere] * 8,
         out_specs=vmem,
         scratch_shapes=[
             pltpu.VMEM((rows, ao, ao), jnp.bfloat16),
@@ -244,10 +267,14 @@
             pltpu.VMEM((dev, per, DB * BLK), jnp.bfloat16),
             pltpu.VMEM((lmos, DB * BLK), jnp.float32),
             pltpu.VMEM((lmos, ao), jnp.bfloat16),
-            pltpu.VMEM((lmos * blocks, rows, BLK), jnp.float32),
+            pltpu.VMEM((lmos * (blocks * rows + 4), BLK), jnp.float32),
             pltpu.VMEM((dev, USED, rows, BLK), jnp.bfloat16),
+            pltpu.VMEM((dev, USED, rows, BLK), jnp.bfloat16),
+            pltpu.VMEM((per, PB, BLK, npao), jnp.bfloat16),
+            pltpu.VMEM((USED * BLK, per * npao), jnp.bfloat16),
             pltpu.SemaphoreType.DMA((rows,)),
             pltpu.SemaphoreType.DMA((6,)),
+            pltpu.SemaphoreType.DMA,
             pltpu.SemaphoreType.REGULAR((dev,)),
             pltpu.SemaphoreType.DMA((dev,)),
             pltpu.SemaphoreType.DMA((dev,)),
@@ -260,25 +287,27 @@
         name="exchange",
     )(*(
         pltpu.with_memory_space_constraint(x, pltpu.HBM)
-        for x in (aux_ints, lmo_coef, ao_domain.T, ao_count.reshape(1, lmos), pao_domain.T, pao_count, owner_order)
+        for x in (
+            aux_ints, lmo_coef, ao_domain.T, ao_count.reshape(1, lmos), pao_domain.T, pao_count,
+            owner_order, pao_coef.reshape(per, PB, BLK, npao),
+        )
     ))
-    pair, metric = pl.pallas_call(
-        functools.partial(contract, n_lmo, per),
+    return pl.pallas_call(
+        contract,
         out_shape=(
             jax.ShapeDtypeStruct((per, dev * rows, npao), jnp.bfloat16),
             jax.ShapeDtypeStruct((per, npao, npao), jnp.float32),
         ),
-        in_specs=[vmem, vmem, smem, smem],
+        in_specs=[vmem],
         out_specs=(anywhere, anywhere),
         scratch_shapes=[
-            pltpu.VMEM((per, dev * rows, npao), jnp.bfloat16),
             pltpu.VMEM((per, npao, npao), jnp.float32),
-            pltpu.SemaphoreType.DMA((per, 2)),
+            pltpu.SemaphoreType.DMA,
+            pltpu.SemaphoreType.DMA((per,)),
         ],
-        compiler_params=pltpu.CompilerParams(vmem_limit_bytes=24 * 2**20),
+        compiler_params=pltpu.CompilerParams(vmem_limit_bytes=16 * 2**20),
         name="contract",
-    )(recv, pao_coef, pao_count, owner_order)
-    return pair, metric
+    )(pair)
 
 
 def solution(mesh):

time: 30.8 us -> 29.4 us (0.955)
  Pallas kernels: 29.9 us -> 28.6 us
    pallas_call x1, Pallas kernels: 2.89 us -> 1.26 us  [shards(): pl.pallas_call(contract, out_shape=(jax.ShapeDtypeStruct((per, dev * rows...]
    pallas_call x1, Pallas kernels: 27.1 us -> 27.4 us  [shards(): pl.pallas_call(functools.partial(exchange, n_aux, n_lmo, plane), out_shap...]
where the time goes in v3:
time: 29.4 us; the launch traced here: 29.3 us
  Pallas kernels  28.6 us (97%)
  between operations  0.64 us (2%)
    pallas_call x1, Pallas kernels, shards(): pl.pallas_call(functools.partial(exchange, n_aux, n_lmo, plane), out_shap...  27.4 us
    pallas_call x1, Pallas kernels, shards(): pl.pallas_call(contract, out_shape=(jax.ShapeDtypeStruct((per, dev * rows...  1.26 us

profile of v3, /device:TPU:13, one launch (start us, length us, event | category | flops | bytes accessed | tf_op | source)
XLA Modules:
  0.0 29.3 jit_solution(10917478875873466011)
XLA Ops:
  0.6 27.4 %exchange.1.pair = bf16[4,256,256]{2,1,0:T(8,128)(2,1)S(1)} custom-call(bf16[8,768,768]{2,1,0:T(8,128)(2,1)} %aux_hbm.1, bf16[4,384]{1,0:T(4,128)(2,1)} %lmo_hbm.1, s32[3,128]{1,0:T(4,128)} %bitcast.5, s32[1,128]{1,0:T(1,128)} %bitcast.7, s32[3,128]{1,0:T(4,128)} %bitcast.6, s32[128]{0:T(128)} %pao_cnt_hbm.1, s32[128]{0:T(128)} %order_hbm.1, ...), custom_call_target="tpu_custom_call" | custom-call | tf_op jit(solution)/shard_map/exchange/pallas_call | solution.py:253
  28.0 1.3 %contract.1 = (bf16[4,256,256]{2,1,0:T(8,128)(2,1)}, f32[4,256,256]{2,1,0:T(8,128)}) custom-call(bf16[4,256,256]{2,1,0:T(8,128)(2,1)S(1)} %exchange.1.pair), custom_call_target="tpu_custom_call" | custom-call | tf_op jit(solution)/shard_map/contract/pallas_call | solution.py:295

commit v4 on v3

--- a/solution.py
+++ b/solution.py
@@ -177,12 +177,6 @@
     pack(me, recv.at[me])
     out_copy(me, target(dev - 2)).start()
 
-    @pl.loop(0, dev - 1)
-    def _(t):
-        d = target(t)
-        coef_copy(d, d).wait_send()
-        out_copy(d, d).wait_send()
-
     npao = pao.shape[3]
     pao_load.wait()
     start = jnp.int32(0)
@@ -216,11 +210,19 @@
                 here, pao_slots[:, g * npao:(g + 1) * npao], preferred_element_type=jnp.float32
             ).astype(jnp.bfloat16)
 
-    project(jnp.where(my_plane == 0, 1, 0) if planes > 1 else my_plane)
-    if planes > 1:
-        project(my_plane)
-    for i in range(1, planes - 1):
-        project(jnp.where(i >= my_plane, i + 1, i))
+    def drain():
+        @pl.loop(0, dev - 1)
+        def _(t):
+            d = target(t)
+            coef_copy(d, d).wait_send()
+            out_copy(d, d).wait_send()
+
+    arrivals = [jnp.where(my_plane == 0, 1, 0), my_plane] if planes > 1 else [my_plane]
+    arrivals += [jnp.where(i >= my_plane, i + 1, i) for i in range(1, planes - 1)]
+    for n, i in enumerate(arrivals):
+        if n == planes - 1:
+            drain()
+        project(i)
 
 
 def contract(pair, pair_out, metric_out, metric, pair_sem, metric_sem):

time: 29.4 us -> 30 us (1.020)
  Pallas kernels: 28.6 us -> 29.2 us
    pallas_call x1, Pallas kernels: 27.4 us -> 28 us  [shards(): pl.pallas_call(functools.partial(exchange, n_aux, n_lmo, plane), out_shap...]
where the time goes in v4:
time: 30 us; the launch traced here: 29.9 us
  Pallas kernels  29.2 us (97%)
  between operations  0.64 us (2%)
    pallas_call x1, Pallas kernels, shards(): pl.pallas_call(functools.partial(exchange, n_aux, n_lmo, plane), out_shap...  28 us
    pallas_call x1, Pallas kernels, shards(): pl.pallas_call(contract, out_shape=(jax.ShapeDtypeStruct((per, dev * rows...  1.26 us

profile of v4, /device:TPU:13, one launch (start us, length us, event | category | flops | bytes accessed | tf_op | source)
XLA Modules:
  0.0 29.9 jit_solution(9636655784233426434)
XLA Ops:
  0.6 28.0 %exchange.1.pair = bf16[4,256,256]{2,1,0:T(8,128)(2,1)S(1)} custom-call(bf16[8,768,768]{2,1,0:T(8,128)(2,1)} %aux_hbm.1, bf16[4,384]{1,0:T(4,128)(2,1)} %lmo_hbm.1, s32[3,128]{1,0:T(4,128)} %bitcast.5, s32[1,128]{1,0:T(1,128)} %bitcast.7, s32[3,128]{1,0:T(4,128)} %bitcast.6, s32[128]{0:T(128)} %pao_cnt_hbm.1, s32[128]{0:T(128)} %order_hbm.1, ...), custom_call_target="tpu_custom_call" | custom-call | tf_op jit(solution)/shard_map/exchange/pallas_call | solution.py:255
  28.6 1.3 %contract.1 = (bf16[4,256,256]{2,1,0:T(8,128)(2,1)}, f32[4,256,256]{2,1,0:T(8,128)}) custom-call(bf16[4,256,256]{2,1,0:T(8,128)(2,1)S(1)} %exchange.1.pair), custom_call_target="tpu_custom_call" | custom-call | tf_op jit(solution)/shard_map/contract/pallas_call | solution.py:297

commit v5 on v3

--- a/solution.py
+++ b/solution.py
@@ -35,10 +35,20 @@
         return (d // n_lmo, lax.rem(d, n_lmo))
 
     barrier = pltpu.get_barrier_semaphore()
-
-    @pl.loop(me + 1, dev)
-    def _(d):
-        pl.semaphore_signal(barrier, inc=1, device_id=coords(d), device_id_type=MESH)
+    before = dev - plane
+    in_last = my_plane == planes - 1
+
+    def others(first, last, act):
+        @pl.loop(first, last)
+        def _(d):
+            @pl.when(d != me)
+            def _():
+                act(d)
+
+    others(
+        jnp.where(in_last, before, 0), dev,
+        lambda d: pl.semaphore_signal(barrier, inc=1, device_id=coords(d), device_id_type=MESH),
+    )
 
     small = [
         pltpu.make_async_copy(src, dst, in_sem.at[n])
@@ -61,33 +71,31 @@
     def coef_copy(slot, d):
         return pltpu.make_async_remote_copy(
             src_ref=lmo_ref, dst_ref=coef_all.at[slot],
-            send_sem=coef_send.at[d], recv_sem=coef_recv.at[slot],
+            send_sem=coef_send, recv_sem=coef_recv,
             device_id=coords(d), device_id_type=MESH,
         )
 
-    @pl.when(me > 0)
+    @pl.when(in_last)
     def _():
-        pl.semaphore_wait(barrier, me)
-
-    @pl.loop(0, me)
-    def _(d):
-        pl.semaphore_signal(entered.at[me], inc=1, device_id=coords(d), device_id_type=MESH)
+        pl.semaphore_wait(barrier, dev - 1)
+
+        @pl.loop(0, before)
+        def _(d):
+            pl.semaphore_signal(entered.at[me], inc=1, device_id=coords(d), device_id_type=MESH)
+
+    if planes > 1:
+        @pl.when(jnp.logical_not(in_last))
+        def _():
+            pl.semaphore_wait(barrier, before - 1)
 
     small[0].wait()
-
-    @pl.loop(0, me)
-    def _(d):
-        coef_copy(me, d).start()
+    for i in range(planes - 2, -1, -1):
+        others(i * plane, (i + 1) * plane, lambda d: coef_copy(me, d).start())
+    others(before, jnp.where(in_last, dev, before), lambda d: coef_copy(me, d).start())
 
     coef_all[me] = lmo_ref[...]
     for copy in small[1:]:
         copy.wait()
-
-    def greet(first, last):
-        @pl.loop(first, last)
-        def _(d):
-            pl.semaphore_wait(entered.at[d], 1)
-            coef_copy(me, d).start()
 
     eye = lax.broadcasted_iota(jnp.int32, (lmos, lmos), 0) == lax.broadcasted_iota(
         jnp.int32, (lmos, lmos), 1
@@ -98,23 +106,27 @@
         column = jnp.sum(jnp.where(eye, block, 0.0), axis=1, keepdims=True)
         where_to.append(jnp.broadcast_to(column, (lmos, BLK)))
 
-    first = me + 1
-    for p in range(max(rows, planes)):
-        if p < planes:
-            last = jnp.minimum(first + plane, dev)
-            greet(first, last)
-            first = last
-        if p < rows:
-            load(p).wait()
-            aux_t[p] = aux[p].T
-
-    @pl.loop(0, me)
+    def turn(p):
+        load(p).wait()
+        aux_t[p] = aux[p].T
+
+    for p in range(rows // 2):
+        turn(p)
+
+    @pl.loop(before, jnp.where(in_last, before, dev))
     def _(d):
-        coef_copy(d, d).wait_recv()
-
-    @pl.loop(me + 1, dev)
-    def _(d):
-        coef_copy(d, d).wait_recv()
+        pl.semaphore_wait(entered.at[d], 1)
+        coef_copy(me, d).start()
+
+    for p in range(rows // 2, rows):
+        turn(p)
+
+    all_coefs = pltpu.make_async_remote_copy(
+        src_ref=coef_all.at[pl.ds(0, dev - 1)], dst_ref=coef_all.at[pl.ds(0, dev - 1)],
+        send_sem=coef_send, recv_sem=coef_recv,
+        device_id=coords(me), device_id_type=MESH,
+    )
+    all_coefs.wait_recv()
 
     for d in range(dev):
         coef32[d * per:(d + 1) * per, :] = coef_all[d].astype(jnp.float32)
@@ -153,16 +165,31 @@
     def out_copy(slot, d):
         return pltpu.make_async_remote_copy(
             src_ref=send.at[d], dst_ref=recv.at[slot],
-            send_sem=out_send.at[d], recv_sem=out_recv.at[slot],
+            send_sem=out_send, recv_sem=out_recv.at[slot // plane],
             device_id=coords(d), device_id_type=MESH,
         )
+
+    def rows_of(first, count, sem):
+        return pltpu.make_async_remote_copy(
+            src_ref=send.at[pl.ds(first, count)], dst_ref=recv.at[pl.ds(first, count)],
+            send_sem=out_send, recv_sem=sem,
+            device_id=coords(me), device_id_type=MESH,
+        )
+
+    half_way = planes // 2
 
     def target(t):
         i, j = t // plane, lax.rem(t, plane)
-        own = i == planes - 1
-        other = jnp.where(i >= my_plane, i + 1, i)
+        down = planes - 1 - i
+        other = jnp.where(
+            my_plane < half_way,
+            jnp.where(down <= my_plane, down - 1, down),
+            jnp.where(i >= my_plane, i + 1, i),
+        )
+        if planes > 2:
+            other = jnp.where(in_last, jnp.where(i == 0, planes - 2, i - 1), other)
         return jnp.where(
-            own,
+            i >= planes - 1,
             my_plane * plane + lax.rem(seat + 1 + j, plane),
             other * plane + lax.rem(seat + j, plane),
         )
@@ -176,12 +203,6 @@
 
     pack(me, recv.at[me])
     out_copy(me, target(dev - 2)).start()
-
-    @pl.loop(0, dev - 1)
-    def _(t):
-        d = target(t)
-        coef_copy(d, d).wait_send()
-        out_copy(d, d).wait_send()
 
     npao = pao.shape[3]
     pao_load.wait()
@@ -196,16 +217,10 @@
             )
         start = start + count
 
-    def project(i):
-        @pl.loop(0, plane)
-        def _(j):
-            d = i * plane + j
-
-            @pl.when(d != me)
-            def _():
-                out_copy(d, d).wait_recv()
-
+    def project(n, i):
         first = pl.multiple_of(i * plane, plane)
+        own = n == 0
+        rows_of(first, plane - own, out_recv.at[i]).wait_recv()
         here = jnp.concatenate([
             recv[pl.ds(first, plane), s].astype(jnp.float32).reshape(plane * rows, BLK).astype(jnp.bfloat16)
             for s in range(USED)
@@ -216,11 +231,19 @@
                 here, pao_slots[:, g * npao:(g + 1) * npao], preferred_element_type=jnp.float32
             ).astype(jnp.bfloat16)
 
-    project(jnp.where(my_plane == 0, 1, 0) if planes > 1 else my_plane)
+    last = jnp.where(my_plane < half_way, half_way, half_way - 1)
+    low, high = jnp.minimum(my_plane, last), jnp.maximum(my_plane, last)
+    arrivals = [my_plane]
+    for n in range(planes - 2):
+        i = planes - 1 - n
+        i = jnp.where(i <= high, i - 1, i)
+        arrivals.append(jnp.where(i <= low, i - 1, i))
     if planes > 1:
-        project(my_plane)
-    for i in range(1, planes - 1):
-        project(jnp.where(i >= my_plane, i + 1, i))
+        arrivals.append(last)
+    for n, i in enumerate(arrivals):
+        project(n, i)
+    all_coefs.wait_send()
+    rows_of(0, dev - 1, out_recv.at[0]).wait_send()
 
 
 def contract(pair, pair_out, metric_out, metric, pair_sem, metric_sem):
@@ -276,10 +299,10 @@
             pltpu.SemaphoreType.DMA((6,)),
             pltpu.SemaphoreType.DMA,
             pltpu.SemaphoreType.REGULAR((dev,)),
-            pltpu.SemaphoreType.DMA((dev,)),
-            pltpu.SemaphoreType.DMA((dev,)),
-            pltpu.SemaphoreType.DMA((dev,)),
-            pltpu.SemaphoreType.DMA((dev,)),
+            pltpu.SemaphoreType.DMA,
+            pltpu.SemaphoreType.DMA,
+            pltpu.SemaphoreType.DMA,
+            pltpu.SemaphoreType.DMA((dev // plane,)),
         ],
         compiler_params=pltpu.CompilerParams(
             collective_id=0, has_side_effects=True, vmem_limit_bytes=48 * 2**20

time: 29.4 us -> 27.9 us (0.949)
  Pallas kernels: 28.6 us -> 27.1 us
    pallas_call x1, Pallas kernels: 27.4 us -> 25.8 us  [shards(): pl.pallas_call(functools.partial(exchange, n_aux, n_lmo, plane), out_shap...]
where the time goes in v5:
time: 27.9 us; the launch traced here: 27.7 us
  Pallas kernels  27.1 us (97%)
  between operations  0.64 us (2%)
    pallas_call x1, Pallas kernels, shards(): pl.pallas_call(functools.partial(exchange, n_aux, n_lmo, plane), out_shap...  25.8 us
    pallas_call x1, Pallas kernels, shards(): pl.pallas_call(contract, out_shape=(jax.ShapeDtypeStruct((per, dev * rows...  1.26 us

profile of v5, /device:TPU:13, one launch (start us, length us, event | category | flops | bytes accessed | tf_op | source)
XLA Modules:
  0.0 27.7 jit_solution(185802401672020921)
XLA Ops:
  0.6 25.8 %exchange.1.pair = bf16[4,256,256]{2,1,0:T(8,128)(2,1)S(1)} custom-call(bf16[8,768,768]{2,1,0:T(8,128)(2,1)} %aux_hbm.1, bf16[4,384]{1,0:T(4,128)(2,1)} %lmo_hbm.1, s32[3,128]{1,0:T(4,128)} %bitcast.5, s32[1,128]{1,0:T(1,128)} %bitcast.7, s32[3,128]{1,0:T(4,128)} %bitcast.6, s32[128]{0:T(128)} %pao_cnt_hbm.1, s32[128]{0:T(128)} %order_hbm.1, ...), custom_call_target="tpu_custom_call" | custom-call | tf_op jit(solution)/shard_map/exchange/pallas_call | solution.py:276
  26.5 1.3 %contract.1 = (bf16[4,256,256]{2,1,0:T(8,128)(2,1)}, f32[4,256,256]{2,1,0:T(8,128)}) custom-call(bf16[4,256,256]{2,1,0:T(8,128)(2,1)S(1)} %exchange.1.pair), custom_call_target="tpu_custom_call" | custom-call | tf_op jit(solution)/shard_map/contract/pallas_call | solution.py:318

commit v6 on v5

--- a/solution.py
+++ b/solution.py
@@ -45,11 +45,6 @@
             def _():
                 act(d)
 
-    others(
-        jnp.where(in_last, before, 0), dev,
-        lambda d: pl.semaphore_signal(barrier, inc=1, device_id=coords(d), device_id_type=MESH),
-    )
-
     small = [
         pltpu.make_async_copy(src, dst, in_sem.at[n])
         for n, (src, dst) in enumerate((
@@ -59,6 +54,19 @@
     ]
     for copy in small:
         copy.start()
+
+    @pl.when(in_last)
+    def _():
+        for j in range(1, plane):
+            d = before + lax.rem(seat + j, plane)
+            pl.semaphore_signal(barrier, inc=1, device_id=coords(d), device_id_type=MESH)
+
+    if planes > 1:
+        @pl.when(jnp.logical_not(in_last))
+        def _():
+            for t in range(1, dev):
+                d = lax.rem(me + t, dev)
+                pl.semaphore_signal(barrier, inc=1, device_id=coords(d), device_id_type=MESH)
 
     def load(p):
         return pltpu.make_async_copy(aux_hbm.at[p], aux.at[p], aux_sem.at[p])
@@ -150,16 +158,21 @@
 
     def pack(d, dst):
         lmo = [order[d * per + j] for j in range(per)]
-        cnt = [pao_cnt[i] for i in lmo]
+        ends, end = [], jnp.int32(0)
+        for j in range(per - 1):
+            end = end + pao_cnt[lmo[j]] - 1
+            ends.append(end)
         for s in range(USED):
-            i, k = lmo[0], jnp.int32(s)
-            start = jnp.int32(0)
-            for j in range(1, per):
-                start = start + cnt[j - 1]
-                past = s >= start
-                i = jnp.where(past, lmo[j], i)
-                k = jnp.where(past, s - start, k)
-            row = i * pitch + pao_dom[jnp.minimum(k, PB - 1), i] * rows
+            if s < per:
+                i, k = lmo[s], 0
+            else:
+                i, k = lmo[0], jnp.int32(s - per + 1)
+                for j in range(1, per):
+                    past = s - per >= ends[j - 1]
+                    i = jnp.where(past, lmo[j], i)
+                    k = jnp.where(past, s - per + 1 - ends[j - 1], k)
+                k = jnp.minimum(k, PB - 1)
+            row = i * pitch + pao_dom[k, i] * rows
             dst[s] = half[pl.ds(row, rows), :].astype(jnp.bfloat16)
 
     def out_copy(slot, d):
@@ -208,36 +221,39 @@
     pao_load.wait()
     start = jnp.int32(0)
     for g in range(per):
-        count = pao_cnt[order[me * per + g]]
-        for s in range(USED):
+        more = pao_cnt[order[me * per + g]] - 1
+        pao_slots[g, :BLK] = pao[g, 0]
+        for s in range(USED - per):
             k = s - start
-            tile = pao[g, jnp.clip(k, 0, PB - 1)]
-            pao_slots[s * BLK:(s + 1) * BLK, g * npao:(g + 1) * npao] = jnp.where(
-                (k >= 0) & (k < count), tile, jnp.zeros_like(tile)
+            tile = pao[g, jnp.clip(k + 1, 0, PB - 1)]
+            pao_slots[g, (s + 1) * BLK:(s + 2) * BLK] = jnp.where(
+                (k >= 0) & (k < more), tile, jnp.zeros_like(tile)
             )
-        start = start + count
+        start = start + more
 
     def project(n, i):
         first = pl.multiple_of(i * plane, plane)
         own = n == 0
         rows_of(first, plane - own, out_recv.at[i]).wait_recv()
-        here = jnp.concatenate([
+        here = [
             recv[pl.ds(first, plane), s].astype(jnp.float32).reshape(plane * rows, BLK).astype(jnp.bfloat16)
             for s in range(USED)
-        ], axis=1)
+        ]
         to = pl.multiple_of(i * (plane * rows), plane * rows)
         for g in range(per):
             pair[g, pl.ds(to, plane * rows), :] = jnp.dot(
-                here, pao_slots[:, g * npao:(g + 1) * npao], preferred_element_type=jnp.float32
+                jnp.concatenate([here[g]] + here[per:], axis=1), pao_slots[g],
+                preferred_element_type=jnp.float32,
             ).astype(jnp.bfloat16)
 
-    last = jnp.where(my_plane < half_way, half_way, half_way - 1)
+    last = jnp.where(my_plane < half_way, planes - 1, half_way - 1)
     low, high = jnp.minimum(my_plane, last), jnp.maximum(my_plane, last)
     arrivals = [my_plane]
     for n in range(planes - 2):
         i = planes - 1 - n
         i = jnp.where(i <= high, i - 1, i)
-        arrivals.append(jnp.where(i <= low, i - 1, i))
+        i = jnp.where(i <= low, i - 1, i)
+        arrivals.append(jnp.where(my_plane < half_way, jnp.where(n >= my_plane, n + 1, n), i))
     if planes > 1:
         arrivals.append(last)
     for n, i in enumerate(arrivals):
@@ -294,7 +310,7 @@
             pltpu.VMEM((dev, USED, rows, BLK), jnp.bfloat16),
             pltpu.VMEM((dev, USED, rows, BLK), jnp.bfloat16),
             pltpu.VMEM((per, PB, BLK, npao), jnp.bfloat16),
-            pltpu.VMEM((USED * BLK, per * npao), jnp.bfloat16),
+            pltpu.VMEM((per, (USED - per + 1) * BLK, npao), jnp.bfloat16),
             pltpu.SemaphoreType.DMA((rows,)),
             pltpu.SemaphoreType.DMA((6,)),
             pltpu.SemaphoreType.DMA,

time: 27.9 us -> 26.3 us (0.943)
  Pallas kernels: 27.1 us -> 25.5 us
    pallas_call x1, Pallas kernels: 25.8 us -> 24.3 us  [shards(): pl.pallas_call(functools.partial(exchange, n_aux, n_lmo, plane), out_shap...]
where the time goes in v6:
time: 26.3 us; the launch traced here: 26.2 us
  Pallas kernels  25.5 us (97%)
  between operations  0.64 us (2%)
    pallas_call x1, Pallas kernels, shards(): pl.pallas_call(functools.partial(exchange, n_aux, n_lmo, plane), out_shap...  24.3 us
    pallas_call x1, Pallas kernels, shards(): pl.pallas_call(contract, out_shape=(jax.ShapeDtypeStruct((per, dev * rows...  1.25 us

profile of v6, /device:TPU:13, one launch (start us, length us, event | category | flops | bytes accessed | tf_op | source)
XLA Modules:
  0.0 26.2 jit_solution(18011203354800416026)
XLA Ops:
  0.6 24.3 %exchange.1.pair = bf16[4,256,256]{2,1,0:T(8,128)(2,1)S(1)} custom-call(bf16[8,768,768]{2,1,0:T(8,128)(2,1)} %aux_hbm.1, bf16[4,384]{1,0:T(4,128)(2,1)} %lmo_hbm.1, s32[3,128]{1,0:T(4,128)} %bitcast.5, s32[1,128]{1,0:T(1,128)} %bitcast.7, s32[3,128]{1,0:T(4,128)} %bitcast.6, s32[128]{0:T(128)} %pao_cnt_hbm.1, s32[128]{0:T(128)} %order_hbm.1, ...), custom_call_target="tpu_custom_call" | custom-call | tf_op jit(solution)/shard_map/exchange/pallas_call | solution.py:292
  24.9 1.3 %contract.1 = (bf16[4,256,256]{2,1,0:T(8,128)(2,1)}, f32[4,256,256]{2,1,0:T(8,128)}) custom-call(bf16[4,256,256]{2,1,0:T(8,128)(2,1)S(1)} %exchange.1.pair), custom_call_target="tpu_custom_call" | custom-call | tf_op jit(solution)/shard_map/contract/pallas_call | solution.py:334

commit v7 on v6

--- a/solution.py
+++ b/solution.py
@@ -11,6 +11,8 @@
 DB = 3
 PB = 3
 USED = 8
+PARTS = 2
+EARLY = 8
 MESH = pl.DeviceIdType.MESH
 
 
@@ -144,19 +146,9 @@
             total = jnp.where(where_to[k] == b, coef32[:, k * BLK:(k + 1) * BLK], total)
         dense[:, b * BLK:(b + 1) * BLK] = total.astype(jnp.bfloat16)
 
-    wide = 2
-    for p in range(rows):
-        for b in range(0, blocks, wide):
-            out = jnp.dot(
-                dense[...], aux_t[p, :, b * BLK:(b + wide) * BLK],
-                preferred_element_type=jnp.float32,
-            )
-            for c in range(wide):
-                half[pl.ds((b + c) * rows + p, lmos, stride=pitch), :] = (
-                    out[:, c * BLK:(c + 1) * BLK]
-                )
-
-    def pack(d, dst):
+    part = rows // PARTS
+
+    def pack(d, dst, parts):
         lmo = [order[d * per + j] for j in range(per)]
         ends, end = [], jnp.int32(0)
         for j in range(per - 1):
@@ -173,11 +165,13 @@
                     k = jnp.where(past, s - per + 1 - ends[j - 1], k)
                 k = jnp.minimum(k, PB - 1)
             row = i * pitch + pao_dom[k, i] * rows
-            dst[s] = half[pl.ds(row, rows), :].astype(jnp.bfloat16)
-
-    def out_copy(slot, d):
+            for h in parts:
+                dst[h, s] = half[pl.ds(row + h * part, part), :].astype(jnp.bfloat16)
+
+    def out_copy(slot, d, h=None):
         return pltpu.make_async_remote_copy(
-            src_ref=send.at[d], dst_ref=recv.at[slot],
+            src_ref=send.at[d] if h is None else send.at[d, h],
+            dst_ref=recv.at[slot] if h is None else recv.at[slot, h],
             send_sem=out_send, recv_sem=out_recv.at[slot // plane],
             device_id=coords(d), device_id_type=MESH,
         )
@@ -193,28 +187,53 @@
 
     def target(t):
         i, j = t // plane, lax.rem(t, plane)
-        down = planes - 1 - i
+        rest = i - (planes - half_way)
         other = jnp.where(
             my_plane < half_way,
-            jnp.where(down <= my_plane, down - 1, down),
+            jnp.where(rest < 0, i + half_way, jnp.where(rest >= my_plane, rest + 1, rest)),
             jnp.where(i >= my_plane, i + 1, i),
         )
-        if planes > 2:
-            other = jnp.where(in_last, jnp.where(i == 0, planes - 2, i - 1), other)
         return jnp.where(
             i >= planes - 1,
             my_plane * plane + lax.rem(seat + 1 + j, plane),
             other * plane + lax.rem(seat + j, plane),
         )
 
-    pack(target(0), send.at[target(0)])
-
-    @pl.loop(0, dev - 2)
+    wide = 2
+
+    def transform(p):
+        for b in range(0, blocks, wide):
+            out = jnp.dot(
+                dense[...], aux_t[p, :, b * BLK:(b + wide) * BLK],
+                preferred_element_type=jnp.float32,
+            )
+            for c in range(wide):
+                half[pl.ds((b + c) * rows + p, lmos, stride=pitch), :] = (
+                    out[:, c * BLK:(c + 1) * BLK]
+                )
+
+    held = None
+    for h in range(PARTS):
+        for p in range(h * part, (h + 1) * part):
+            transform(p)
+            if held is not None:
+                held.start()
+                held = None
+        for t in range(EARLY):
+            d = target(t)
+            pack(d, send.at[d], (h,))
+            if held is not None:
+                held.start()
+            held = out_copy(me, d, h)
+    pack(target(EARLY), send.at[target(EARLY)], range(PARTS))
+    held.start()
+
+    @pl.loop(EARLY, dev - 2)
     def _(t):
-        pack(target(t + 1), send.at[target(t + 1)])
+        pack(target(t + 1), send.at[target(t + 1)], range(PARTS))
         out_copy(me, target(t)).start()
 
-    pack(me, recv.at[me])
+    pack(me, recv.at[me], range(PARTS))
     out_copy(me, target(dev - 2)).start()
 
     npao = pao.shape[3]
@@ -236,7 +255,9 @@
         own = n == 0
         rows_of(first, plane - own, out_recv.at[i]).wait_recv()
         here = [
-            recv[pl.ds(first, plane), s].astype(jnp.float32).reshape(plane * rows, BLK).astype(jnp.bfloat16)
+            jnp.concatenate(
+                [recv[pl.ds(first, plane), h, s].astype(jnp.float32) for h in range(PARTS)], axis=1
+            ).reshape(plane * rows, BLK).astype(jnp.bfloat16)
             for s in range(USED)
         ]
         to = pl.multiple_of(i * (plane * rows), plane * rows)
@@ -246,14 +267,14 @@
                 preferred_element_type=jnp.float32,
             ).astype(jnp.bfloat16)
 
-    last = jnp.where(my_plane < half_way, planes - 1, half_way - 1)
+    last = jnp.where(in_last, half_way - 1, my_plane + 1)
     low, high = jnp.minimum(my_plane, last), jnp.maximum(my_plane, last)
     arrivals = [my_plane]
     for n in range(planes - 2):
         i = planes - 1 - n
         i = jnp.where(i <= high, i - 1, i)
         i = jnp.where(i <= low, i - 1, i)
-        arrivals.append(jnp.where(my_plane < half_way, jnp.where(n >= my_plane, n + 1, n), i))
+        arrivals.append(i)
     if planes > 1:
         arrivals.append(last)
     for n, i in enumerate(arrivals):
@@ -307,8 +328,8 @@
             pltpu.VMEM((lmos, DB * BLK), jnp.float32),
             pltpu.VMEM((lmos, ao), jnp.bfloat16),
             pltpu.VMEM((lmos * (blocks * rows + 4), BLK), jnp.float32),
-            pltpu.VMEM((dev, USED, rows, BLK), jnp.bfloat16),
-            pltpu.VMEM((dev, USED, rows, BLK), jnp.bfloat16),
+            pltpu.VMEM((dev, PARTS, USED, rows // PARTS, BLK), jnp.bfloat16),
+            pltpu.VMEM((dev, PARTS, USED, rows // PARTS, BLK), jnp.bfloat16),
             pltpu.VMEM((per, PB, BLK, npao), jnp.bfloat16),
             pltpu.VMEM((per, (USED - per + 1) * BLK, npao), jnp.bfloat16),
             pltpu.SemaphoreType.DMA((rows,)),

time: 26.3 us -> 25.4 us (0.966)
  Pallas kernels: 25.5 us -> 24.5 us
    pallas_call x1, Pallas kernels: 24.3 us -> 23.2 us  [shards(): pl.pallas_call(functools.partial(exchange, n_aux, n_lmo, plane), out_shap...]
where the time goes in v7:
time: 25.4 us; the launch traced here: 25.1 us
  Pallas kernels  24.5 us (96%)
  between operations  0.64 us (3%)
    pallas_call x1, Pallas kernels, shards(): pl.pallas_call(functools.partial(exchange, n_aux, n_lmo, plane), out_shap...  23.2 us
    pallas_call x1, Pallas kernels, shards(): pl.pallas_call(contract, out_shape=(jax.ShapeDtypeStruct((per, dev * rows...  1.26 us

profile of v7, /device:TPU:13, one launch (start us, length us, event | category | flops | bytes accessed | tf_op | source)
XLA Modules:
  0.0 25.1 jit_solution(3068018609096994298)
XLA Ops:
  0.6 23.2 %exchange.1.pair = bf16[4,256,256]{2,1,0:T(8,128)(2,1)S(1)} custom-call(bf16[8,768,768]{2,1,0:T(8,128)(2,1)} %aux_hbm.1, bf16[4,384]{1,0:T(4,128)(2,1)} %lmo_hbm.1, s32[3,128]{1,0:T(4,128)} %bitcast.5, s32[1,128]{1,0:T(1,128)} %bitcast.7, s32[3,128]{1,0:T(4,128)} %bitcast.6, s32[128]{0:T(128)} %pao_cnt_hbm.1, s32[128]{0:T(128)} %order_hbm.1, ...), custom_call_target="tpu_custom_call" | custom-call | tf_op jit(solution)/shard_map/exchange/pallas_call | solution.py:313
  23.9 1.3 %contract.1 = (bf16[4,256,256]{2,1,0:T(8,128)(2,1)}, f32[4,256,256]{2,1,0:T(8,128)}) custom-call(bf16[4,256,256]{2,1,0:T(8,128)(2,1)S(1)} %exchange.1.pair), custom_call_target="tpu_custom_call" | custom-call | tf_op jit(solution)/shard_map/contract/pallas_call | solution.py:355

commit v8 on v7

--- a/solution.py
+++ b/solution.py
@@ -12,7 +12,7 @@
 PB = 3
 USED = 8
 PARTS = 2
-EARLY = 8
+EARLY = 6
 MESH = pl.DeviceIdType.MESH
 
 
@@ -20,7 +20,7 @@
     n_aux, n_lmo, plane,
     aux_hbm, lmo_hbm, ao_dom_hbm, ao_cnt_hbm, pao_dom_hbm, pao_cnt_hbm, order_hbm, pao_hbm, pair,
     aux, aux_t, lmo_ref, ao_dom, ao_cnt, pao_dom, pao_cnt, order,
-    coef_all, coef32, dense, half, send, recv, pao, pao_slots,
+    coef_all, coef32, dense, half, tab, send, recv, pao, pao_slots,
     aux_sem, in_sem, pao_sem, entered, coef_send, coef_recv, out_send, out_recv,
 ):
     dev = n_aux * n_lmo
@@ -116,44 +116,29 @@
         column = jnp.sum(jnp.where(eye, block, 0.0), axis=1, keepdims=True)
         where_to.append(jnp.broadcast_to(column, (lmos, BLK)))
 
-    def turn(p):
-        load(p).wait()
-        aux_t[p] = aux[p].T
-
-    for p in range(rows // 2):
-        turn(p)
-
-    @pl.loop(before, jnp.where(in_last, before, dev))
-    def _(d):
-        pl.semaphore_wait(entered.at[d], 1)
-        coef_copy(me, d).start()
-
-    for p in range(rows // 2, rows):
-        turn(p)
-
-    all_coefs = pltpu.make_async_remote_copy(
-        src_ref=coef_all.at[pl.ds(0, dev - 1)], dst_ref=coef_all.at[pl.ds(0, dev - 1)],
-        send_sem=coef_send, recv_sem=coef_recv,
-        device_id=coords(me), device_id_type=MESH,
-    )
-    all_coefs.wait_recv()
-
-    for d in range(dev):
-        coef32[d * per:(d + 1) * per, :] = coef_all[d].astype(jnp.float32)
-    for b in range(blocks):
-        total = jnp.zeros((lmos, BLK), jnp.float32)
-        for k in range(DB):
-            total = jnp.where(where_to[k] == b, coef32[:, k * BLK:(k + 1) * BLK], total)
-        dense[:, b * BLK:(b + 1) * BLK] = total.astype(jnp.bfloat16)
-
-    part = rows // PARTS
-
-    def pack(d, dst, parts):
+    half_way = planes // 2
+
+    def target(t):
+        i, j = t // plane, lax.rem(t, plane)
+        rest = i - (planes - half_way)
+        other = jnp.where(
+            my_plane < half_way,
+            jnp.where(rest < 0, i + half_way, jnp.where(rest >= my_plane, rest + 1, rest)),
+            jnp.where(i >= my_plane, i + 1, i),
+        )
+        return jnp.where(
+            i >= planes - 1,
+            my_plane * plane + lax.rem(seat + 1 + j, plane),
+            other * plane + lax.rem(seat + j, plane),
+        )
+
+    def slot_rows(d):
         lmo = [order[d * per + j] for j in range(per)]
         ends, end = [], jnp.int32(0)
         for j in range(per - 1):
             end = end + pao_cnt[lmo[j]] - 1
             ends.append(end)
+        found = []
         for s in range(USED):
             if s < per:
                 i, k = lmo[s], 0
@@ -164,7 +149,46 @@
                     i = jnp.where(past, lmo[j], i)
                     k = jnp.where(past, s - per + 1 - ends[j - 1], k)
                 k = jnp.minimum(k, PB - 1)
-            row = i * pitch + pao_dom[k, i] * rows
+            found.append(i * pitch + pao_dom[k, i] * rows)
+        return found
+
+    def turn(p):
+        load(p).wait()
+        aux_t[p] = aux[p].T
+        for t in range(p * EARLY // rows, (p + 1) * EARLY // rows):
+            for s, row in enumerate(slot_rows(target(t))):
+                tab[t * USED + s] = row
+
+    for p in range(rows // 2):
+        turn(p)
+
+    @pl.loop(before, jnp.where(in_last, before, dev))
+    def _(d):
+        pl.semaphore_wait(entered.at[d], 1)
+        coef_copy(me, d).start()
+
+    for p in range(rows // 2, rows):
+        turn(p)
+
+    all_coefs = pltpu.make_async_remote_copy(
+        src_ref=coef_all.at[pl.ds(0, dev - 1)], dst_ref=coef_all.at[pl.ds(0, dev - 1)],
+        send_sem=coef_send, recv_sem=coef_recv,
+        device_id=coords(me), device_id_type=MESH,
+    )
+    all_coefs.wait_recv()
+
+    for d in range(dev):
+        coef32[d * per:(d + 1) * per, :] = coef_all[d].astype(jnp.float32)
+    for b in range(blocks):
+        total = jnp.zeros((lmos, BLK), jnp.float32)
+        for k in range(DB):
+            total = jnp.where(where_to[k] == b, coef32[:, k * BLK:(k + 1) * BLK], total)
+        dense[:, b * BLK:(b + 1) * BLK] = total.astype(jnp.bfloat16)
+
+    part = rows // PARTS
+
+    def pack(d, dst, parts, found=None):
+        for s, row in enumerate(found if found else slot_rows(d)):
             for h in parts:
                 dst[h, s] = half[pl.ds(row + h * part, part), :].astype(jnp.bfloat16)
 
@@ -181,22 +205,6 @@
             src_ref=send.at[pl.ds(first, count)], dst_ref=recv.at[pl.ds(first, count)],
             send_sem=out_send, recv_sem=sem,
             device_id=coords(me), device_id_type=MESH,
-        )
-
-    half_way = planes // 2
-
-    def target(t):
-        i, j = t // plane, lax.rem(t, plane)
-        rest = i - (planes - half_way)
-        other = jnp.where(
-            my_plane < half_way,
-            jnp.where(rest < 0, i + half_way, jnp.where(rest >= my_plane, rest + 1, rest)),
-            jnp.where(i >= my_plane, i + 1, i),
-        )
-        return jnp.where(
-            i >= planes - 1,
-            my_plane * plane + lax.rem(seat + 1 + j, plane),
-            other * plane + lax.rem(seat + j, plane),
         )
 
     wide = 2
@@ -221,7 +229,7 @@
                 held = None
         for t in range(EARLY):
             d = target(t)
-            pack(d, send.at[d], (h,))
+            pack(d, send.at[d], (h,), [tab[t * USED + s] for s in range(USED)])
             if held is not None:
                 held.start()
             held = out_copy(me, d, h)
@@ -328,6 +336,7 @@
             pltpu.VMEM((lmos, DB * BLK), jnp.float32),
             pltpu.VMEM((lmos, ao), jnp.bfloat16),
             pltpu.VMEM((lmos * (blocks * rows + 4), BLK), jnp.float32),
+            pltpu.SMEM((EARLY * USED,), jnp.int32),
             pltpu.VMEM((dev, PARTS, USED, rows // PARTS, BLK), jnp.bfloat16),
             pltpu.VMEM((dev, PARTS, USED, rows // PARTS, BLK), jnp.bfloat16),
             pltpu.VMEM((per, PB, BLK, npao), jnp.bfloat16),

time: 25.4 us -> 25.5 us (level)
  no operation moved by 1% of the time
where the time goes in v8:
time: 25.5 us; the launch traced here: 25.2 us
  Pallas kernels  24.5 us (96%)
  between operations  0.64 us (3%)
    pallas_call x1, Pallas kernels, shards(): pl.pallas_call(functools.partial(exchange, n_aux, n_lmo, plane), out_shap...  23.3 us
    pallas_call x1, Pallas kernels, shards(): pl.pallas_call(contract, out_shape=(jax.ShapeDtypeStruct((per, dev * rows...  1.25 us

profile of v8, /device:TPU:13, one launch (start us, length us, event | category | flops | bytes accessed | tf_op | source)
XLA Modules:
  0.0 25.2 jit_solution(2074474284276826847)
XLA Ops:
  0.6 23.3 %exchange.1.pair = bf16[4,256,256]{2,1,0:T(8,128)(2,1)S(1)} custom-call(bf16[8,768,768]{2,1,0:T(8,128)(2,1)} %aux_hbm.1, bf16[4,384]{1,0:T(4,128)(2,1)} %lmo_hbm.1, s32[3,128]{1,0:T(4,128)} %bitcast.5, s32[1,128]{1,0:T(1,128)} %bitcast.7, s32[3,128]{1,0:T(4,128)} %bitcast.6, s32[128]{0:T(128)} %pao_cnt_hbm.1, s32[128]{0:T(128)} %order_hbm.1, ...), custom_call_target="tpu_custom_call" | custom-call | tf_op jit(solution)/shard_map/exchange/pallas_call | solution.py:321
  23.9 1.3 %contract.1 = (bf16[4,256,256]{2,1,0:T(8,128)(2,1)}, f32[4,256,256]{2,1,0:T(8,128)}) custom-call(bf16[4,256,256]{2,1,0:T(8,128)(2,1)S(1)} %exchange.1.pair), custom_call_target="tpu_custom_call" | custom-call | tf_op jit(solution)/shard_map/contract/pallas_call | solution.py:364
